TPU v7x, 32 devices: a whole 2x2x4 slice. The times are simulated.
32 devices in a mesh: gz: 8 (over z, y), gy: 4 (over x, core).
Axes of the slice: x: 2, y: 2, z: 4, core: 2. Of those that a mesh axis runs over, the one named last changes fastest.
Arguments:
- orbitals: bfloat16 [96, 96, 96, 256], P('gz', 'gy'), may hold values from -6 to 6
- pair_list: int32 [64, 2], replicated, may hold values from 0 to 255
- box_anchor: int32 [256, 3], replicated, may hold values from 0 to 95
- pair_live: int32 [64], replicated, may hold values from 0 to 1, as said below
Outputs:
- gradient: float32 [96, 96, 96, 256], P('gz', 'gy')
Inputs may be any that keep to these rules, and one draw needn't show every extreme that they name: `pair_live`: in each owner's block of 2 slots the live slots come first; at least one slot of every block is live, some block has all 2 live, and some other block has exactly one live.
All inputs are finite; a program needn't handle non-finite values.
Results may differ from a plain program's by a relative error of at most 0.0035.
Values may be sent and summed in bfloat16 or wider, within the bound.
A program may use at most 192 MiB of HBM per device.

v0:
```python
import jax
import jax.numpy as jnp
from jax import lax
from jax.sharding import PartitionSpec as P

B = 64


def poisson_box(density):
    side = density.shape[-1]
    index = jnp.arange(1, side + 1).astype(jnp.float32)
    table = jnp.sqrt(2.0 / (side + 1.0)) * jnp.sin(
        jnp.pi * index[:, None] * index[None, :] / (side + 1.0)
    )
    eigen = 2.0 - 2.0 * jnp.cos(jnp.pi * index / (side + 1.0))
    denom = eigen[:, None, None] + eigen[None, :, None] + eigen[None, None, :]
    hp = lax.Precision.HIGHEST

    def apply_all(field):
        field = jnp.einsum("...abc,ai->...ibc", field, table, precision=hp)
        field = jnp.einsum("...ibc,bj->...ijc", field, table, precision=hp)
        return jnp.einsum("...ijc,ck->...ijk", field, table, precision=hp)

    return apply_all(apply_all(density) / denom)


def body(orbitals, pair_list, box_anchor, pair_live):
    depth, rows, across, norb = orbitals.shape
    n_gz = lax.axis_size("gz")
    n_gy = lax.axis_size("gy")
    owners = n_gz * n_gy
    pairs = pair_list.shape[0]
    per_dev = pairs // owners
    slots = 2 * per_dev
    side = B
    extent = depth * n_gz
    firsts = pair_list[:, 0]
    chosen = jnp.take(orbitals, pair_list.reshape(-1), axis=3)
    width = chosen.shape[2]
    outgoing = chosen.reshape(depth, rows, width, n_gz, n_gy, slots)
    flat_send = outgoing.reshape(depth, rows, width, owners, slots)
    incoming = lax.all_to_all(
        flat_send, ("gz", "gy"), split_axis=3, concat_axis=3, tiled=True
    ).reshape(depth, rows, width, n_gz, n_gy, slots)
    grids = jnp.transpose(incoming, (5, 3, 0, 4, 1, 2)).reshape(per_dev, 2, extent, extent, width)
    owner = lax.axis_index(("gz", "gy"))
    mine = lax.dynamic_slice_in_dim(pair_list, owner * per_dev, per_dev, 0)
    live = lax.dynamic_slice_in_dim(pair_live, owner * per_dev, per_dev, 0)
    anchors = box_anchor[mine[:, 0]]

    def cut_box(grid, anchor):
        grid = jnp.roll(grid, -anchor[0], axis=0)
        grid = jnp.roll(grid, -anchor[1], axis=1)
        grid = jnp.roll(grid, -anchor[2], axis=2)
        return grid[:side, :side, :side]

    def both_boxes(pair_grids, anchor):
        return jax.vmap(cut_box, in_axes=(0, None))(pair_grids, anchor)

    boxes = jax.vmap(both_boxes)(grids, anchors)
    left = boxes[:, 0].astype(jnp.float32)
    right = boxes[:, 1].astype(jnp.float32)
    potential = poisson_box(left * right)
    weight = live.astype(jnp.float32)[:, None, None, None]
    term = (potential * right * weight).astype(jnp.bfloat16)

    def place_box(box, anchor):
        pad_x = across - side
        grid = jnp.pad(box, ((0, extent - side), (0, extent - side), (0, pad_x)))
        grid = jnp.roll(grid, anchor[0], axis=0)
        grid = jnp.roll(grid, anchor[1], axis=1)
        grid = jnp.roll(grid, anchor[2], axis=2)
        return grid

    placed = jax.vmap(place_box)(term, anchors)
    back_send = jnp.transpose(
        placed.reshape(per_dev, n_gz, depth, n_gy, rows, width), (2, 4, 5, 1, 3, 0)
    )
    flat_back = back_send.reshape(depth, rows, width, owners, per_dev)
    back = lax.all_to_all(flat_back, ("gz", "gy"), split_axis=3, concat_axis=3, tiled=True)
    contrib = back.reshape(depth, rows, width, pairs)
    selector = (firsts[:, None] == jnp.arange(norb)[None, :]).astype(jnp.bfloat16)
    action = jnp.dot(contrib.reshape(-1, pairs), selector, preferred_element_type=jnp.float32)
    action_low = action.astype(jnp.bfloat16)
    flat = orbitals.reshape(-1, norb)
    partial_tiles = lax.dot_general(
        flat, action_low, (((0,), (0,)), ((), ())), preferred_element_type=jnp.float32
    )
    summed = lax.psum(partial_tiles, ("gz", "gy"))
    tiles = (summed / (float(B) ** 3 / 4.0)).astype(jnp.bfloat16)
    gradient = action - jnp.dot(flat, tiles, preferred_element_type=jnp.float32)
    return gradient.reshape(depth, rows, across, norb)


def solution(mesh):
    return jax.shard_map(
        body,
        mesh=mesh,
        in_specs=(P("gz", "gy", None, None), P(), P(), P()),
        out_specs=P("gz", "gy", None, None),
        check_vma=False,
    )
```

profile of v0, /device:TPU:0, one launch (start us, length us, event | category | flops | bytes accessed | tf_op | source)
XLA Modules:
  0.0 842.0 jit_solution(8082996493727971002)
XLA Ops:
  7.5 22.4 %copy.44 = bf16[12,24,96,256]{2,1,0,3:T(8,128)(2,1)} copy(bf16[12,24,96,256]{3,2,1,0:T(8,128)(2,1)} %param.4) | data formatting | bytes 28311552 | tf_op args[0]
  29.9 13.6 %gather_fusion = bf16[128,12,24,96]{3,2,1,0:T(8,128)(2,1)} fusion(bf16[12,24,96,256]{2,1,0,3:T(8,128)(2,1)} %copy.44, s32[1024]{0:T(1024)S(1)} %pad_clamp_fusion.1), kind=kCustom, calls=%fused_computation | custom fusion | bytes 14156288 | tf_op jit(solution)/shard_map/jit(_take)/gather | solution.py:38
  43.5 9.6 %copy.45 = bf16[12,24,96,128]{2,1,3,0:T(8,128)(2,1)} copy(bf16[12,24,96,128]{2,1,0,3:T(8,128)(2,1)} %bitcast.113) | data formatting | bytes 14155776 | tf_op jit(solution)/shard_map/jit(_take)/gather | solution.py:38
  53.2 8.6 %broadcast_select_fusion = bf16[12,24,96,32,4]{2,1,4,3,0:T(8,128)(2,1)} fusion(bf16[12,24,96,32,4]{2,1,4,3,0:T(8,128)(2,1)} %bitcast.112, pred[32,4]{1,0:T(8,128)(4,1)S(1)} %compare_and_fusion), kind=kLoop, calls=%fused_computation.24 | loop fusion | flops 3538944 | bytes 14155904 | tf_op jit(solution)/shard_map/jit(_take)/select_n | solution.py:38
  61.7 10.2 %copy.46 = bf16[12,24,96,32,4]{2,1,4,0,3:T(8,128)(2,1)} copy(bf16[12,24,96,32,4]{2,1,4,3,0:T(8,128)(2,1)} %broadcast_select_fusion) | data formatting | bytes 14155776 | tf_op jit(solution)/shard_map/jit(_take)/select_n | solution.py:38
  71.9 7.9 all-to-all-start
  81.8 206.9 %all-to-all-done = bf16[12,24,96,32,4]{2,1,4,0,3:T(8,128)(2,1)} async-done(((bf16[12,24,96,32,4]{2,1,4,0,3:T(8,128)(2,1)}), bf16[12,24,96,32,4]{2,1,4,0,3:T(8,128)(2,1)}, u32[]{:S(2)}, u32[]{:S(2)}) %all-to-all-start) | async-done | bytes 7077920 | tf_op jit(solution)/shard_map/all_to_all | solution.py:42
  288.7 10.2 %copy.48 = bf16[4,8,12,4,24,96]{5,4,3,2,1,0:T(8,128)(2,1)} copy(bf16[4,8,12,4,24,96]{5,4,0,2,3,1:T(8,128)(2,1)} %bitcast.9) | data formatting | bytes 14155776 | tf_op jit(solution)/shard_map/transpose | solution.py:45
  298.9 16.0 %pad_maximum_fusion = bf16[2,2,192,96,96]{4,3,2,1,0:T(8,128)(2,1)} fusion(bf16[2,2,96,96,96]{4,3,2,1,0:T(8,128)(2,1)} %bitcast.111), kind=kLoop, calls=%fused_computation.16 | loop fusion | flops 7077888 | bytes 21233664 | tf_op jit(solution)/shard_map/vmap(vmap(jit(_roll_dynamic)))/concatenate | solution.py:52
  314.9 5.1 broadcast.265.clone.1
  320.1 14.5 %while.6 = (s32[]{:T(128)}, bf16[2,2,192,96,96]{4,3,2,1,0:T(8,128)(2,1)}, s32[2,4]{1,0:T(2,128)S(1)}, bf16[2,2,96,96,96]{4,3,2,1,0:T(8,128)(2,1)}, s32[]{:T(128)}) while((s32[]{:T(128)}, bf16[2,2,192,96,96]{4,3,2,1,0:T(8,128)(2,1)}, s32[2,4]{1,0:T(2,128)S(1)}, bf16[2,2,96,96,96]{4,3,2,1,0:T(8,128)(2,1)}, s32[]{:T(128)}) %tuple.99), condition=%wide.while_cond, body=%wide.while_body.sunk | while | flops 2 | bytes 9438833 | solution.py:52
  320.7 6.7 dynamic-slice_dynamic-update-slice_fusion.10
  328.1 6.5 dynamic-slice_dynamic-update-slice_fusion.10
  334.6 18.2 %pad_maximum_fusion.1 = bf16[2,2,96,192,96]{4,3,2,1,0:T(8,128)(2,1)} fusion(bf16[2,2,96,96,96]{4,3,2,1,0:T(8,128)(2,1)} %get-tuple-element.12), kind=kLoop, calls=%fused_computation.17 | loop fusion | flops 28311552 | bytes 21233664 | tf_op jit(solution)/shard_map/vmap(vmap(jit(_roll_dynamic)))/concatenate | solution.py:53
  352.8 5.1 broadcast.265
  357.9 18.6 %while.7 = (s32[]{:T(128)}, bf16[2,2,96,192,96]{4,3,2,1,0:T(8,128)(2,1)}, s32[2,4]{1,0:T(2,128)S(1)}, bf16[2,2,96,96,96]{4,3,2,1,0:T(8,128)(2,1)}, s32[]{:T(128)}) while((s32[]{:T(128)}, bf16[2,2,96,192,96]{4,3,2,1,0:T(8,128)(2,1)}, s32[2,4]{1,0:T(2,128)S(1)}, bf16[2,2,96,96,96]{4,3,2,1,0:T(8,128)(2,1)}, s32[]{:T(128)}) %tuple.102), condition=%wide.while_cond.1, body=%wide.while_body.1.sunk | while | flops 2 | bytes 9438833 | solution.py:53
  358.6 8.7 %dynamic-slice_dynamic-update-slice_fusion.11 = bf16[2,2,96,96,96]{4,3,2,1,0:T(8,128)(2,1)} fusion(bf16[2,2,96,96,96]{4,3,2,1,0:T(8,128)(2,1)} %get-tuple-element.323, s32[]{:T(128)} %get-tuple-element.320, bf16[2,2,96,192,96]{4,3,2,1,0:T(8,128)(2,1)} %get-tuple-element.326, s32[]{:T(128)} %bitcast.98, s32[]{:T(128)} %bitcast.99), kind=kLoop, calls=%fused_computation.4.clone.1 | loop fusion | bytes 9438720 | tf_op jit(solution)/shard_map/vmap(vmap(jit(_roll_dynamic)))/gather
  368.0 8.6 %dynamic-slice_dynamic-update-slice_fusion.11 = bf16[2,2,96,96,96]{4,3,2,1,0:T(8,128)(2,1)} fusion(bf16[2,2,96,96,96]{4,3,2,1,0:T(8,128)(2,1)} %get-tuple-element.323, s32[]{:T(128)} %get-tuple-element.320, bf16[2,2,96,192,96]{4,3,2,1,0:T(8,128)(2,1)} %get-tuple-element.326, s32[]{:T(128)} %bitcast.98, s32[]{:T(128)} %bitcast.99), kind=kLoop, calls=%fused_computation.4.clone.1 | loop fusion | bytes 9438720 | tf_op jit(solution)/shard_map/vmap(vmap(jit(_roll_dynamic)))/gather
  376.5 20.0 %pad_maximum_fusion.2 = bf16[2,2,96,96,192]{4,3,2,1,0:T(8,128)(2,1)} fusion(bf16[2,2,96,96,96]{4,3,2,1,0:T(8,128)(2,1)} %get-tuple-element.20), kind=kLoop, calls=%fused_computation.18 | loop fusion | flops 28311552 | bytes 21233664 | tf_op jit(solution)/shard_map/vmap(vmap(jit(_roll_dynamic)))/concatenate | solution.py:54
  396.6 18.8 %while.8 = (s32[]{:T(128)}, bf16[2,2,96,96,192]{4,3,2,1,0:T(8,128)(2,1)}, s32[2,4]{1,0:T(2,128)S(1)}, bf16[2,2,96,96,96]{4,3,2,0,1:T(8,128)(2,1)}, s32[]{:T(128)}) while((s32[]{:T(128)}, bf16[2,2,96,96,192]{4,3,2,1,0:T(8,128)(2,1)}, s32[2,4]{1,0:T(2,128)S(1)}, bf16[2,2,96,96,96]{4,3,2,0,1:T(8,128)(2,1)}, s32[]{:T(128)}) %tuple.105), condition=%wide.while_cond.2, body=%wide.while_body.2.sunk | while | flops 2 | bytes 9438833 | solution.py:54
  397.2 8.7 %bitcast_dynamic-update-slice_fusion.2 = bf16[2,2,96,96,96]{4,3,2,0,1:T(8,128)(2,1)} fusion(bf16[2,2,96,96,96]{4,3,2,0,1:T(8,128)(2,1)} %get-tuple-element.338, s32[]{:T(128)} %get-tuple-element.335, bf16[2,2,96,96,192]{4,3,2,1,0:T(8,128)(2,1)} %get-tuple-element.341, s32[]{:T(128)} %bitcast.101, s32[]{:T(128)} %bitcast.102), kind=kLoop, calls=%fused_computation.6.clone.1 | loop fusion | bytes 9438720 | tf_op jit(solution)/shard_map/vmap(vmap(jit(_roll_dynamic)))/gather
  406.5 8.8 %bitcast_dynamic-update-slice_fusion.2 = bf16[2,2,96,96,96]{4,3,2,0,1:T(8,128)(2,1)} fusion(bf16[2,2,96,96,96]{4,3,2,0,1:T(8,128)(2,1)} %get-tuple-element.338, s32[]{:T(128)} %get-tuple-element.335, bf16[2,2,96,96,192]{4,3,2,1,0:T(8,128)(2,1)} %get-tuple-element.341, s32[]{:T(128)} %bitcast.101, s32[]{:T(128)} %bitcast.102), kind=kLoop, calls=%fused_computation.6.clone.1 | loop fusion | bytes 9438720 | tf_op jit(solution)/shard_map/vmap(vmap(jit(_roll_dynamic)))/gather
  418.6 6.4 fusion.17
  425.0 6.6 fusion.13
  431.7 3.8 fusion.23
  435.5 6.4 fusion.20
  441.9 6.8 fusion.9
  448.7 5.3 fusion.4
  454.8 4.5 pad_maximum_fusion.3
  462.1 10.2 %while.9 = (s32[]{:T(128)}, bf16[2,192,96,96]{3,2,1,0:T(8,128)(2,1)}, s32[2,4]{1,0:T(2,128)S(1)}, bf16[2,96,96,96]{3,2,1,0:T(8,128)(2,1)}, s32[]{:T(128)}) while((s32[]{:T(128)}, bf16[2,192,96,96]{3,2,1,0:T(8,128)(2,1)}, s32[2,4]{1,0:T(2,128)S(1)}, bf16[2,96,96,96]{3,2,1,0:T(8,128)(2,1)}, s32[]{:T(128)}) %tuple.108), condition=%wide.while_cond.3, body=%wide.while_body.3.sunk | while | flops 2 | bytes 4720241 | solution.py:70
  462.7 4.5 dynamic-slice_dynamic-update-slice_fusion.12
  467.8 4.5 dynamic-slice_dynamic-update-slice_fusion.12
  472.2 10.1 %pad_maximum_fusion.4 = bf16[2,96,192,96]{3,2,1,0:T(8,128)(2,1)} fusion(bf16[2,96,96,96]{3,2,1,0:T(8,128)(2,1)} %get-tuple-element.36), kind=kLoop, calls=%fused_computation.22 | loop fusion | flops 14155776 | bytes 10616832 | tf_op jit(solution)/shard_map/vmap(jit(_roll_dynamic))/concatenate | solution.py:71
  485.0 12.3 %while.10 = (s32[]{:T(128)}, bf16[2,96,192,96]{3,2,1,0:T(8,128)(2,1)}, s32[2,4]{1,0:T(2,128)S(1)}, bf16[2,96,96,96]{3,2,1,0:T(8,128)(2,1)}, s32[]{:T(128)}) while((s32[]{:T(128)}, bf16[2,96,192,96]{3,2,1,0:T(8,128)(2,1)}, s32[2,4]{1,0:T(2,128)S(1)}, bf16[2,96,96,96]{3,2,1,0:T(8,128)(2,1)}, s32[]{:T(128)}) %tuple.111), condition=%wide.while_cond.4, body=%wide.while_body.4.sunk | while | flops 2 | bytes 4720241 | solution.py:71
  485.7 5.5 dynamic-slice_dynamic-update-slice_fusion.13
  491.8 5.5 dynamic-slice_dynamic-update-slice_fusion.13
  497.4 11.6 %pad_maximum_fusion.5 = bf16[2,96,96,192]{3,2,1,0:T(8,128)(2,1)} fusion(bf16[2,96,96,96]{3,2,1,0:T(8,128)(2,1)} %get-tuple-element.44), kind=kLoop, calls=%fused_computation.23 | loop fusion | flops 14155776 | bytes 10616832 | tf_op jit(solution)/shard_map/vmap(jit(_roll_dynamic))/concatenate | solution.py:72
  511.7 12.9 %while.11 = (s32[]{:T(128)}, bf16[2,96,96,192]{3,2,1,0:T(8,128)(2,1)}, s32[2,4]{1,0:T(2,128)S(1)}, bf16[2,96,96,96]{3,2,1,0:T(8,128)(2,1)}, s32[]{:T(128)}) while((s32[]{:T(128)}, bf16[2,96,96,192]{3,2,1,0:T(8,128)(2,1)}, s32[2,4]{1,0:T(2,128)S(1)}, bf16[2,96,96,96]{3,2,1,0:T(8,128)(2,1)}, s32[]{:T(128)}) %tuple.114), condition=%wide.while_cond.5, body=%wide.while_body.5.sunk | while | flops 2 | bytes 4720241 | solution.py:72
  512.3 5.8 dynamic-slice_dynamic-update-slice_fusion.14
  518.8 5.8 dynamic-slice_dynamic-update-slice_fusion.14
  524.6 3.7 copy.61
  535.5 105.1 %all-to-all-done.1 = bf16[12,24,96,32,2]{2,1,4,0,3:T(8,128)(2,1)} async-done(((bf16[12,24,96,32,2]{2,1,4,0,3:T(8,128)(2,1)}), bf16[12,24,96,32,2]{2,1,4,0,3:T(8,128)(2,1)}, u32[]{:S(2)}, u32[]{:S(2)}) %all-to-all-start.1) | async-done | bytes 3538976 | tf_op jit(solution)/shard_map/all_to_all | solution.py:80
  640.6 5.3 copy.63
  646.0 8.1 reshape_reshape.4
  654.1 12.0 %fusion.32 = f32[27648,256]{1,0:T(8,128)} fusion(bf16[27648,64]{0,1:T(8,128)(2,1)S(1)} %reshape_reshape.4, s32[64]{0:T(128)S(1)} %slice_bitcast_fusion), kind=kOutput, calls=%fused_computation.49 | convolution fusion | flops 905986048 | bytes 31850752 | tf_op jit(solution)/shard_map/dot_general | solution.py:83
  666.1 17.6 %fusion.28 = f32[256,256]{0,1:T(8,128)} fusion(bf16[27648,256]{1,0:T(8,128)(2,1)} %bitcast.109, f32[27648,256]{1,0:T(8,128)} %fusion.32), kind=kOutput, calls=%fused_computation.44 | convolution fusion | flops 3630956544 | bytes 42729472 | tf_op jit(solution)/shard_map/dot_general | solution.py:86
  683.8 126.0 %all-reduce.7.cloned.1.call-done = f32[256,256]{0,1:T(8,128)} async-done(((f32[256,256]{0,1:T(8,128)}), f32[256,256]{0,1:T(8,128)}) %all-reduce.7.cloned.1.call-update) | async-done | bytes 262160 | tf_op jit(solution)/shard_map/psum | solution.py:89
  809.7 25.2 %fusion = f32[27648,256]{1,0:T(8,128)} fusion(f32[27648,256]{1,0:T(8,128)} %fusion.32, bf16[27648,256]{1,0:T(8,128)(2,1)} %bitcast.110, f32[256,256]{0,1:T(8,128)} %all-reduce.7.cloned.1.call-done), kind=kOutput, calls=%fused_computation.15 | convolution fusion | flops 3631087616 | bytes 71041024 | tf_op jit(solution)/shard_map/dot_general | solution.py:91
  (63 shorter events, 29.7 us)
Async XLA Ops:
  71.9 7.9 copy-start
  71.9 8.9 %copy-start.2 = (s32[64]{0:T(128)S(1)}, s32[64]{0:T(128)}, u32[]{:S(2)}) copy-start(s32[64]{0:T(128)} %param.7) | copy-start | bytes 772
  71.9 216.8 %all-to-all-start = ((bf16[12,24,96,32,4]{2,1,4,0,3:T(8,128)(2,1)}), bf16[12,24,96,32,4]{2,1,4,0,3:T(8,128)(2,1)}, u32[]{:S(2)}, u32[]{:S(2)}) async-start(bf16[12,24,96,32,4]{2,1,4,0,3:T(8,128)(2,1)} %copy.46), calls=%async_computation | async-start | bytes 18874368 | tf_op jit(solution)/shard_map/all_to_all | solution.py:42
  528.3 7.2 copy-start.1
  531.9 108.8 %all-to-all-start.1 = ((bf16[12,24,96,32,2]{2,1,4,0,3:T(8,128)(2,1)}), bf16[12,24,96,32,2]{2,1,4,0,3:T(8,128)(2,1)}, u32[]{:S(2)}, u32[]{:S(2)}) async-start(bf16[12,24,96,32,2]{2,1,4,0,3:T(8,128)(2,1)} %copy.62), calls=%async_computation.1 | async-start | bytes 9437184 | tf_op jit(solution)/shard_map/all_to_all | solution.py:80
  535.5 274.3 %all-reduce.7.cloned.1.call-start = ((), (), s32[]{:S(2)}) async-start(), calls=%async_computation.2 | async-start | bytes 524288 | tf_op jit(solution)/shard_map/psum | solution.py:89
Sparse Core Ops, SparseCore 0:
  683.9 125.7 all-reduce.6
where the time goes:
time: 849 us; the launch traced here: 842 us
  waiting for transfers between devices  438 us (52%)
  local copies, waits for them, and re-layouts  195 us (23%)
  other arithmetic  93.4 us (11%)
  matrix products  90.2 us (11%)
  between operations  13.9 us (2%)
  starting transfers between devices  11.5 us (1%)
    all_to_all x1, waiting for transfers between devices, body(): lax.all_to_all(flat_send, ('gz', 'gy'), split_axis=3, concat_axis=3, tile...  207 us
    psum x1, waiting for transfers between devices, body(): summed = lax.psum(partial_tiles, ('gz', 'gy'))  126 us
    all_to_all x1, waiting for transfers between devices, body(): lax.all_to_all(flat_back, ('gz', 'gy'), split_axis=3, concat_axis=3, tile...  105 us
    gather x36, local copies, waits for them, and re-layouts  87.1 us
    unnamed x15, local copies, waits for them, and re-layouts  41.7 us
    dot_general x1, matrix products, body(): gradient = action - jnp.dot(flat, tiles, preferred_element_type=jnp.float32)  25.2 us
    gather x2, local copies, waits for them, and re-layouts, body(): chosen = jnp.take(orbitals, pair_list.reshape(-1), axis=3)  23.2 us
    concatenate x1, other arithmetic, cut_box(): grid = jnp.roll(grid, -anchor[2], axis=2)  20 us
  transfers between devices with their start and end apart: 3, of which 3 were waited for; matrix products, arithmetic and copies ran while one was open for 0% of the time, Pallas kernels for 0%

commit v1 on v0

--- a/solution.py
+++ b/solution.py
@@ -86,7 +86,7 @@
     partial_tiles = lax.dot_general(
         flat, action_low, (((0,), (0,)), ((), ())), preferred_element_type=jnp.float32
     )
-    summed = lax.psum(partial_tiles, ("gz", "gy"))
+    summed = jnp.sum(lax.all_gather(partial_tiles, ("gz", "gy")), axis=0)
     tiles = (summed / (float(B) ** 3 / 4.0)).astype(jnp.bfloat16)
     gradient = action - jnp.dot(flat, tiles, preferred_element_type=jnp.float32)
     return gradient.reshape(depth, rows, across, norb)

time: 849 us -> 816 us (0.961)
  waiting for transfers between devices: 438 us -> 395 us
    psum x1 -> x0, waiting for transfers between devices: 126 us -> none  [body(): summed = lax.psum(partial_tiles, ('gz', 'gy'))]
    all_gather x0 -> x1, waiting for transfers between devices: none -> 83.4 us  [body(): summed = jnp.sum(lax.all_gather(partial_tiles, ('gz', 'gy')), axis=0)]
    unnamed x15 -> x16, local copies, waits for them, and re-layouts: 41.7 us -> 48.5 us
where the time goes in v1:
time: 816 us; the launch traced here: 809 us
  waiting for transfers between devices  395 us (48%)
  local copies, waits for them, and re-layouts  202 us (25%)
  other arithmetic  95.6 us (12%)
  matrix products  90.2 us (11%)
  between operations  13.9 us (2%)
  starting transfers between devices  11.6 us (1%)
    all_to_all x1, waiting for transfers between devices, body(): lax.all_to_all(flat_send, ('gz', 'gy'), split_axis=3, concat_axis=3, tile...  207 us
    all_to_all x1, waiting for transfers between devices, body(): lax.all_to_all(flat_back, ('gz', 'gy'), split_axis=3, concat_axis=3, tile...  105 us
    gather x36, local copies, waits for them, and re-layouts  87.1 us
    all_gather x1, waiting for transfers between devices, body(): summed = jnp.sum(lax.all_gather(partial_tiles, ('gz', 'gy')), axis=0)  83.4 us
    unnamed x16, local copies, waits for them, and re-layouts  48.5 us
    dot_general x1, matrix products, body(): gradient = action - jnp.dot(flat, tiles, preferred_element_type=jnp.float32)  25.2 us
    gather x2, local copies, waits for them, and re-layouts, body(): chosen = jnp.take(orbitals, pair_list.reshape(-1), axis=3)  23.2 us
    concatenate x1, other arithmetic, cut_box(): grid = jnp.roll(grid, -anchor[2], axis=2)  20 us
  transfers between devices with their start and end apart: 3, of which 3 were waited for; matrix products, arithmetic and copies ran while one was open for 0% of the time, Pallas kernels for 0%

profile of v1, /device:TPU:0, one launch (start us, length us, event | category | flops | bytes accessed | tf_op | source)
XLA Modules:
  0.0 808.6 jit_solution(605773581374932261)
XLA Ops:
  7.5 22.4 %copy.44 = bf16[12,24,96,256]{2,1,0,3:T(8,128)(2,1)} copy(bf16[12,24,96,256]{3,2,1,0:T(8,128)(2,1)} %param.4) | data formatting | bytes 28311552 | tf_op args[0]
  29.9 13.6 %gather_fusion = bf16[128,12,24,96]{3,2,1,0:T(8,128)(2,1)} fusion(bf16[12,24,96,256]{2,1,0,3:T(8,128)(2,1)} %copy.44, s32[1024]{0:T(1024)S(1)} %pad_clamp_fusion.1), kind=kCustom, calls=%fused_computation | custom fusion | bytes 14156288 | tf_op jit(solution)/shard_map/jit(_take)/gather | solution.py:38
  43.5 9.6 %copy.45 = bf16[12,24,96,128]{2,1,3,0:T(8,128)(2,1)} copy(bf16[12,24,96,128]{2,1,0,3:T(8,128)(2,1)} %bitcast.118) | data formatting | bytes 14155776 | tf_op jit(solution)/shard_map/jit(_take)/gather | solution.py:38
  53.2 8.6 %broadcast_select_fusion = bf16[12,24,96,32,4]{2,1,4,3,0:T(8,128)(2,1)} fusion(bf16[12,24,96,32,4]{2,1,4,3,0:T(8,128)(2,1)} %bitcast.117, pred[32,4]{1,0:T(8,128)(4,1)S(1)} %compare_and_fusion), kind=kLoop, calls=%fused_computation.24 | loop fusion | flops 3538944 | bytes 14155904 | tf_op jit(solution)/shard_map/jit(_take)/select_n | solution.py:38
  61.7 10.2 %copy.46 = bf16[12,24,96,32,4]{2,1,4,0,3:T(8,128)(2,1)} copy(bf16[12,24,96,32,4]{2,1,4,3,0:T(8,128)(2,1)} %broadcast_select_fusion) | data formatting | bytes 14155776 | tf_op jit(solution)/shard_map/jit(_take)/select_n | solution.py:38
  71.9 8.0 all-to-all-start
  81.9 206.9 %all-to-all-done = bf16[12,24,96,32,4]{2,1,4,0,3:T(8,128)(2,1)} async-done(((bf16[12,24,96,32,4]{2,1,4,0,3:T(8,128)(2,1)}), bf16[12,24,96,32,4]{2,1,4,0,3:T(8,128)(2,1)}, u32[]{:S(2)}, u32[]{:S(2)}) %all-to-all-start) | async-done | bytes 7077920 | tf_op jit(solution)/shard_map/all_to_all | solution.py:42
  288.8 10.2 %copy.48 = bf16[4,8,12,4,24,96]{5,4,3,2,1,0:T(8,128)(2,1)} copy(bf16[4,8,12,4,24,96]{5,4,0,2,3,1:T(8,128)(2,1)} %bitcast.9) | data formatting | bytes 14155776 | tf_op jit(solution)/shard_map/transpose | solution.py:45
  299.0 16.0 %pad_maximum_fusion = bf16[2,2,192,96,96]{4,3,2,1,0:T(8,128)(2,1)} fusion(bf16[2,2,96,96,96]{4,3,2,1,0:T(8,128)(2,1)} %bitcast.116), kind=kLoop, calls=%fused_computation.16 | loop fusion | flops 7077888 | bytes 21233664 | tf_op jit(solution)/shard_map/vmap(vmap(jit(_roll_dynamic)))/concatenate | solution.py:52
  315.0 5.1 broadcast.265.clone.1
  320.1 14.5 %while.6 = (s32[]{:T(128)}, bf16[2,2,192,96,96]{4,3,2,1,0:T(8,128)(2,1)}, s32[2,4]{1,0:T(2,128)S(1)}, bf16[2,2,96,96,96]{4,3,2,1,0:T(8,128)(2,1)}, s32[]{:T(128)}) while((s32[]{:T(128)}, bf16[2,2,192,96,96]{4,3,2,1,0:T(8,128)(2,1)}, s32[2,4]{1,0:T(2,128)S(1)}, bf16[2,2,96,96,96]{4,3,2,1,0:T(8,128)(2,1)}, s32[]{:T(128)}) %tuple.99), condition=%wide.while_cond, body=%wide.while_body.sunk | while | flops 2 | bytes 9438833 | solution.py:52
  320.8 6.7 dynamic-slice_dynamic-update-slice_fusion.10
  328.1 6.5 dynamic-slice_dynamic-update-slice_fusion.10
  334.6 18.2 %pad_maximum_fusion.1 = bf16[2,2,96,192,96]{4,3,2,1,0:T(8,128)(2,1)} fusion(bf16[2,2,96,96,96]{4,3,2,1,0:T(8,128)(2,1)} %get-tuple-element.12), kind=kLoop, calls=%fused_computation.17 | loop fusion | flops 28311552 | bytes 21233664 | tf_op jit(solution)/shard_map/vmap(vmap(jit(_roll_dynamic)))/concatenate | solution.py:53
  352.9 5.1 broadcast.265
  358.0 18.6 %while.7 = (s32[]{:T(128)}, bf16[2,2,96,192,96]{4,3,2,1,0:T(8,128)(2,1)}, s32[2,4]{1,0:T(2,128)S(1)}, bf16[2,2,96,96,96]{4,3,2,1,0:T(8,128)(2,1)}, s32[]{:T(128)}) while((s32[]{:T(128)}, bf16[2,2,96,192,96]{4,3,2,1,0:T(8,128)(2,1)}, s32[2,4]{1,0:T(2,128)S(1)}, bf16[2,2,96,96,96]{4,3,2,1,0:T(8,128)(2,1)}, s32[]{:T(128)}) %tuple.102), condition=%wide.while_cond.1, body=%wide.while_body.1.sunk | while | flops 2 | bytes 9438833 | solution.py:53
  358.7 8.7 %dynamic-slice_dynamic-update-slice_fusion.11 = bf16[2,2,96,96,96]{4,3,2,1,0:T(8,128)(2,1)} fusion(bf16[2,2,96,96,96]{4,3,2,1,0:T(8,128)(2,1)} %get-tuple-element.323, s32[]{:T(128)} %get-tuple-element.320, bf16[2,2,96,192,96]{4,3,2,1,0:T(8,128)(2,1)} %get-tuple-element.326, s32[]{:T(128)} %bitcast.103, s32[]{:T(128)} %bitcast.104), kind=kLoop, calls=%fused_computation.4.clone.1 | loop fusion | bytes 9438720 | tf_op jit(solution)/shard_map/vmap(vmap(jit(_roll_dynamic)))/gather
  368.0 8.6 %dynamic-slice_dynamic-update-slice_fusion.11 = bf16[2,2,96,96,96]{4,3,2,1,0:T(8,128)(2,1)} fusion(bf16[2,2,96,96,96]{4,3,2,1,0:T(8,128)(2,1)} %get-tuple-element.323, s32[]{:T(128)} %get-tuple-element.320, bf16[2,2,96,192,96]{4,3,2,1,0:T(8,128)(2,1)} %get-tuple-element.326, s32[]{:T(128)} %bitcast.103, s32[]{:T(128)} %bitcast.104), kind=kLoop, calls=%fused_computation.4.clone.1 | loop fusion | bytes 9438720 | tf_op jit(solution)/shard_map/vmap(vmap(jit(_roll_dynamic)))/gather
  376.6 20.0 %pad_maximum_fusion.2 = bf16[2,2,96,96,192]{4,3,2,1,0:T(8,128)(2,1)} fusion(bf16[2,2,96,96,96]{4,3,2,1,0:T(8,128)(2,1)} %get-tuple-element.20), kind=kLoop, calls=%fused_computation.18 | loop fusion | flops 28311552 | bytes 21233664 | tf_op jit(solution)/shard_map/vmap(vmap(jit(_roll_dynamic)))/concatenate | solution.py:54
  396.6 18.8 %while.8 = (s32[]{:T(128)}, bf16[2,2,96,96,192]{4,3,2,1,0:T(8,128)(2,1)}, s32[2,4]{1,0:T(2,128)S(1)}, bf16[2,2,96,96,96]{4,3,2,0,1:T(8,128)(2,1)}, s32[]{:T(128)}) while((s32[]{:T(128)}, bf16[2,2,96,96,192]{4,3,2,1,0:T(8,128)(2,1)}, s32[2,4]{1,0:T(2,128)S(1)}, bf16[2,2,96,96,96]{4,3,2,0,1:T(8,128)(2,1)}, s32[]{:T(128)}) %tuple.105), condition=%wide.while_cond.2, body=%wide.while_body.2.sunk | while | flops 2 | bytes 9438833 | solution.py:54
  397.2 8.7 %bitcast_dynamic-update-slice_fusion.2 = bf16[2,2,96,96,96]{4,3,2,0,1:T(8,128)(2,1)} fusion(bf16[2,2,96,96,96]{4,3,2,0,1:T(8,128)(2,1)} %get-tuple-element.338, s32[]{:T(128)} %get-tuple-element.335, bf16[2,2,96,96,192]{4,3,2,1,0:T(8,128)(2,1)} %get-tuple-element.341, s32[]{:T(128)} %bitcast.106, s32[]{:T(128)} %bitcast.107), kind=kLoop, calls=%fused_computation.6.clone.1 | loop fusion | bytes 9438720 | tf_op jit(solution)/shard_map/vmap(vmap(jit(_roll_dynamic)))/gather
  406.6 8.8 %bitcast_dynamic-update-slice_fusion.2 = bf16[2,2,96,96,96]{4,3,2,0,1:T(8,128)(2,1)} fusion(bf16[2,2,96,96,96]{4,3,2,0,1:T(8,128)(2,1)} %get-tuple-element.338, s32[]{:T(128)} %get-tuple-element.335, bf16[2,2,96,96,192]{4,3,2,1,0:T(8,128)(2,1)} %get-tuple-element.341, s32[]{:T(128)} %bitcast.106, s32[]{:T(128)} %bitcast.107), kind=kLoop, calls=%fused_computation.6.clone.1 | loop fusion | bytes 9438720 | tf_op jit(solution)/shard_map/vmap(vmap(jit(_roll_dynamic)))/gather
  418.7 6.4 fusion.17
  425.1 6.6 fusion.13
  431.8 3.8 fusion.23
  435.5 6.4 fusion.20
  442.0 6.8 fusion.9
  448.8 5.3 fusion.4
  454.8 4.5 pad_maximum_fusion.3
  462.1 10.2 %while.9 = (s32[]{:T(128)}, bf16[2,192,96,96]{3,2,1,0:T(8,128)(2,1)}, s32[2,4]{1,0:T(2,128)S(1)}, bf16[2,96,96,96]{3,2,1,0:T(8,128)(2,1)}, s32[]{:T(128)}) while((s32[]{:T(128)}, bf16[2,192,96,96]{3,2,1,0:T(8,128)(2,1)}, s32[2,4]{1,0:T(2,128)S(1)}, bf16[2,96,96,96]{3,2,1,0:T(8,128)(2,1)}, s32[]{:T(128)}) %tuple.108), condition=%wide.while_cond.3, body=%wide.while_body.3.sunk | while | flops 2 | bytes 4720241 | solution.py:70
  462.7 4.5 dynamic-slice_dynamic-update-slice_fusion.12
  467.8 4.5 dynamic-slice_dynamic-update-slice_fusion.12
  472.3 10.1 %pad_maximum_fusion.4 = bf16[2,96,192,96]{3,2,1,0:T(8,128)(2,1)} fusion(bf16[2,96,96,96]{3,2,1,0:T(8,128)(2,1)} %get-tuple-element.36), kind=kLoop, calls=%fused_computation.22 | loop fusion | flops 14155776 | bytes 10616832 | tf_op jit(solution)/shard_map/vmap(jit(_roll_dynamic))/concatenate | solution.py:71
  485.1 12.3 %while.10 = (s32[]{:T(128)}, bf16[2,96,192,96]{3,2,1,0:T(8,128)(2,1)}, s32[2,4]{1,0:T(2,128)S(1)}, bf16[2,96,96,96]{3,2,1,0:T(8,128)(2,1)}, s32[]{:T(128)}) while((s32[]{:T(128)}, bf16[2,96,192,96]{3,2,1,0:T(8,128)(2,1)}, s32[2,4]{1,0:T(2,128)S(1)}, bf16[2,96,96,96]{3,2,1,0:T(8,128)(2,1)}, s32[]{:T(128)}) %tuple.111), condition=%wide.while_cond.4, body=%wide.while_body.4.sunk | while | flops 2 | bytes 4720241 | solution.py:71
  485.7 5.5 dynamic-slice_dynamic-update-slice_fusion.13
  491.8 5.5 dynamic-slice_dynamic-update-slice_fusion.13
  497.5 11.6 %pad_maximum_fusion.5 = bf16[2,96,96,192]{3,2,1,0:T(8,128)(2,1)} fusion(bf16[2,96,96,96]{3,2,1,0:T(8,128)(2,1)} %get-tuple-element.44), kind=kLoop, calls=%fused_computation.23 | loop fusion | flops 14155776 | bytes 10616832 | tf_op jit(solution)/shard_map/vmap(jit(_roll_dynamic))/concatenate | solution.py:72
  511.8 12.9 %while.11 = (s32[]{:T(128)}, bf16[2,96,96,192]{3,2,1,0:T(8,128)(2,1)}, s32[2,4]{1,0:T(2,128)S(1)}, bf16[2,96,96,96]{3,2,1,0:T(8,128)(2,1)}, s32[]{:T(128)}) while((s32[]{:T(128)}, bf16[2,96,96,192]{3,2,1,0:T(8,128)(2,1)}, s32[2,4]{1,0:T(2,128)S(1)}, bf16[2,96,96,96]{3,2,1,0:T(8,128)(2,1)}, s32[]{:T(128)}) %tuple.114), condition=%wide.while_cond.5, body=%wide.while_body.5.sunk | while | flops 2 | bytes 4720241 | solution.py:72
  512.4 5.8 dynamic-slice_dynamic-update-slice_fusion.14
  518.8 5.8 dynamic-slice_dynamic-update-slice_fusion.14
  535.6 105.1 %all-to-all-done.1 = bf16[12,24,96,32,2]{2,1,4,0,3:T(8,128)(2,1)} async-done(((bf16[12,24,96,32,2]{2,1,4,0,3:T(8,128)(2,1)}), bf16[12,24,96,32,2]{2,1,4,0,3:T(8,128)(2,1)}, u32[]{:S(2)}, u32[]{:S(2)}) %all-to-all-start.1) | async-done | bytes 3538976 | tf_op jit(solution)/shard_map/all_to_all | solution.py:80
  640.7 5.3 copy.63
  646.0 8.1 %reshape_reshape.4 = bf16[27648,64]{0,1:T(8,128)(2,1)S(1)} reshape(bf16[12,24,96,32,2]{2,1,0,4,3:T(8,128)(2,1)} %copy.63) | data formatting | bytes 7077888 | tf_op jit(solution)/shard_map/reshape;reshape | solution.py:83
  654.1 12.0 %fusion.32 = f32[27648,256]{1,0:T(8,128)} fusion(bf16[27648,64]{0,1:T(8,128)(2,1)S(1)} %reshape_reshape.4, s32[64]{0:T(128)S(1)} %slice_bitcast_fusion), kind=kOutput, calls=%fused_computation.50 | convolution fusion | flops 905986048 | bytes 31850752 | tf_op jit(solution)/shard_map/dot_general | solution.py:83
  666.2 17.6 %fusion.28 = f32[256,256]{0,1:T(8,128)} fusion(bf16[27648,256]{1,0:T(8,128)(2,1)} %bitcast.114, f32[27648,256]{1,0:T(8,128)} %fusion.32), kind=kOutput, calls=%fused_computation.45 | convolution fusion | flops 3630956544 | bytes 42729472 | tf_op jit(solution)/shard_map/dot_general | solution.py:86
  683.8 83.4 %all-gather.3.cloned.1.call-done = f32[8192,256]{0,1:T(8,128)} async-done(((f32[256,256]{0,1:T(8,128)}), f32[8192,256]{0,1:T(8,128)}) %all-gather.3.cloned.1.call-update) | async-done | bytes 8388624 | tf_op jit(solution)/shard_map/all_gather | solution.py:89
  767.3 6.8 copy.79
  776.3 25.2 %fusion = f32[27648,256]{1,0:T(8,128)} fusion(f32[27648,256]{1,0:T(8,128)} %fusion.32, bf16[27648,256]{1,0:T(8,128)(2,1)} %bitcast.115, f32[256,256]{0,1:T(8,128)S(1)} %bitcast_reduce_fusion), kind=kOutput, calls=%fused_computation.15 | convolution fusion | flops 3631087616 | bytes 71041024 | tf_op jit(solution)/shard_map/dot_general | solution.py:91
  (65 shorter events, 35.6 us)
Async XLA Ops:
  71.9 8.0 copy-start
  71.9 8.9 %copy-start.2 = (s32[64]{0:T(128)S(1)}, s32[64]{0:T(128)}, u32[]{:S(2)}) copy-start(s32[64]{0:T(128)} %param.7) | copy-start | bytes 772
  71.9 216.8 %all-to-all-start = ((bf16[12,24,96,32,4]{2,1,4,0,3:T(8,128)(2,1)}), bf16[12,24,96,32,4]{2,1,4,0,3:T(8,128)(2,1)}, u32[]{:S(2)}, u32[]{:S(2)}) async-start(bf16[12,24,96,32,4]{2,1,4,0,3:T(8,128)(2,1)} %copy.46), calls=%async_computation | async-start | bytes 18874368 | tf_op jit(solution)/shard_map/all_to_all | solution.py:42
  528.3 7.2 copy-start.1
  531.9 108.8 %all-to-all-start.1 = ((bf16[12,24,96,32,2]{2,1,4,0,3:T(8,128)(2,1)}), bf16[12,24,96,32,2]{2,1,4,0,3:T(8,128)(2,1)}, u32[]{:S(2)}, u32[]{:S(2)}) async-start(bf16[12,24,96,32,2]{2,1,4,0,3:T(8,128)(2,1)} %copy.62), calls=%async_computation.1 | async-start | bytes 9437184 | tf_op jit(solution)/shard_map/all_to_all | solution.py:80
  535.5 231.7 %all-gather.3.cloned.1.call-start = ((), (), s32[]{:S(2)}) async-start(), calls=%async_computation.2 | async-start | bytes 8650752 | tf_op jit(solution)/shard_map/all_gather | solution.py:89
Sparse Core Ops, SparseCore 0:
  684.0 83.2 all-gather.2
